TPU v7x, 32 devices: a whole 2x2x4 slice. The times are simulated.
32 devices in a mesh: dp: 8 (over z, x), tensor: 4 (over y, core).
Axes of the slice: x: 2, y: 2, z: 4, core: 2. Of those that a mesh axis runs over, the one named last changes fastest.
Arguments:
- tokens: bfloat16 [8192, 1536], P('dp'), may hold values from -6 to 6
- lengths: int32 [12], replicated, may hold values from 512 to 1024, as said below
- owners: int32 [12], replicated, may hold values from 0 to 7, as said below
- first_gain: float32 [1536], replicated, may hold values from 0.5 to 1.5
- query_weight: bfloat16 [1536, 1536], P(None, 'tensor')
- key_weight: bfloat16 [1536, 768], P(None, 'tensor')
- value_weight: bfloat16 [1536, 768], P(None, 'tensor'), may hold values from -0.15625 to 0.15625
- mixing_weight: bfloat16 [1536, 1536], P(None, 'tensor'), may hold values from -2.5 to 2.5
- second_gain: float32 [1536], replicated, may hold values from 0.5 to 1.5
- gate_weight: bfloat16 [1536, 4096], P(None, 'tensor'), may hold values from -0.15625 to 0.15625
- up_weight: bfloat16 [1536, 4096], P(None, 'tensor'), may hold values from -0.15625 to 0.15625
- down_weight: bfloat16 [1536, 4096], P(None, 'tensor'), may hold values from -0.09375 to 0.09375
- cotangent: bfloat16 [8192, 1536], P('dp'), may hold values from -6 to 6
Outputs:
- layer_output: bfloat16 [8192, 1536], P(('dp', 'tensor'))
- token_grad: bfloat16 [8192, 1536], P(('dp', 'tensor'))
- first_grad: float32 [1536], replicated
- query_grad: float32 [1536, 1536], P('dp', 'tensor')
- key_grad: float32 [1536, 768], P('dp', 'tensor')
- value_grad: float32 [1536, 768], P('dp', 'tensor')
- mixing_grad: float32 [1536, 1536], P('dp', 'tensor')
- second_grad: float32 [1536], replicated
- gate_grad: float32 [1536, 4096], P('dp', 'tensor')
- up_grad: float32 [1536, 4096], P('dp', 'tensor')
- down_grad: float32 [1536, 4096], P('dp', 'tensor')
Inputs may be any that keep to these rules, and one draw needn't show every extreme that they name: `lengths`: the sequences of one index of dp total at most 1024 tokens; one sequence has exactly 1024 tokens and one exactly 512. `owners`: every index of dp holds one or two sequences.
All inputs are finite; a program needn't handle non-finite values.
Results may differ from a plain program's by a relative error of at most 0.023.
Values may be sent and summed in bfloat16 or wider, within the bound.
A program may use at most 192 MiB of HBM per device.

v0:
```python
import jax
import jax.numpy as jnp
import numpy as np
from jax import lax
from jax.experimental import pallas as pl
from jax.experimental.pallas import tpu as pltpu
from jax.sharding import PartitionSpec as P

HD = 96

MESH = pl.DeviceIdType.MESH

epsilon = 1e-05
rope_base = 10000.0


def bits_of(count):
    return tuple(range(count.bit_length() - 1))


def nn(left, right):
    return jnp.dot(left, right, preferred_element_type=jnp.float32)


def nt(left, right):
    return lax.dot_general(left, right, (((1,), (1,)), ((), ())), preferred_element_type=jnp.float32)


def tn(left, right):
    return lax.dot_general(left, right, (((0,), (0,)), ((), ())), preferred_element_type=jnp.float32)


def flip(index, mask):
    result = index
    bit = 0
    while mask >> bit:
        if (mask >> bit) & 1:
            result = result + (1 << bit) * (1 - 2 * lax.rem(lax.div(index, 1 << bit), 2))
        bit += 1
    return result


def span(start, size, step=16):
    return pl.ds(pl.multiple_of(start, step), size)


def greet(peers):
    barrier = pltpu.get_barrier_semaphore()
    for axis, bit in peers:
        index = lax.axis_index(axis)
        pl.semaphore_signal(
            barrier, inc=1, device_id={axis: flip(index, 1 << bit)}, device_id_type=MESH
        )
    pl.semaphore_wait(barrier, len(peers))


def chunk_rows(rows):
    for size in (16,):
        if rows % size == 0:
            return size
    return rows


class Reduce:
    def __init__(self, part, landing, send_sems, recv_sems, axis, order, split=1):
        self.part, self.landing = part, landing
        self.send_sems, self.recv_sems = send_sems, recv_sems
        self.axis, self.order, self.split = axis, order, split
        self.index = lax.axis_index(axis)
        self.rows = part.shape[0] >> len(order)
        self.piece = self.rows // split
        self.copies = {}
        self.lists = []
        base = 0
        for step in range(len(order)):
            kept = [0]
            for bit in reversed(order[step + 1 :]):
                kept = [place | (1 << bit) for place in kept] + kept
            self.lists.append((kept, base))
            base += len(kept) * split

    @staticmethod
    def slots(count, split=1):
        return (count - 1) * split

    def units(self, step):
        kept, _ = self.lists[step]
        return [(j, c) for j in range(len(kept)) for c in range(self.split)]

    def start(self, step, j, c=0):
        kept, base = self.lists[step]
        mask = 1 << self.order[step]
        slot = base + j * self.split + c
        source = flip(self.index, kept[j] | mask) * self.rows + c * self.piece
        copy = pltpu.make_async_remote_copy(
            src_ref=self.part.at[span(source, self.piece)],
            dst_ref=self.landing.at[slot],
            send_sem=self.send_sems.at[slot],
            recv_sem=self.recv_sems.at[slot],
            device_id={self.axis: flip(self.index, mask)},
            device_id_type=MESH,
        )
        copy.start()
        self.copies[slot] = copy

    def arrive(self, step, j, c=0, store=None):
        kept, base = self.lists[step]
        slot = base + j * self.split + c
        self.copies[slot].wait_recv()
        start = flip(self.index, kept[j]) * self.rows + c * self.piece
        size = chunk_rows(self.piece)

        def add(i, carry):
            rows = span(start + i * size, size)
            other = self.landing[slot, span(i * size, size)]
            total = self.part[rows].astype(jnp.float32) + other.astype(jnp.float32)
            if store is None:
                self.part[rows] = total.astype(self.part.dtype)
            else:
                store(c * self.piece + i * size, size, total)
            return carry

        lax.fori_loop(0, self.piece // size, add, 0)
        if step + 1 < len(self.order):
            later, _ = self.lists[step + 1]
            mask = 1 << self.order[step + 1]
            if kept[j] & mask:
                self.start(step + 1, later.index(kept[j] ^ mask), c)

    def start_all(self):
        for j, c in self.units(0):
            self.start(0, j, c)

    def arrive_all(self, step, store=None):
        for j, c in self.units(step):
            self.arrive(step, j, c, store)

    def close(self):
        for copy in self.copies.values():
            copy.wait_send()


class Gather:
    def __init__(self, whole, send_sems, recv_sems, split=1):
        self.whole, self.split = whole, split
        self.send_sems, self.recv_sems = send_sems, recv_sems
        self.index = lax.axis_index("tensor")
        self.rows = whole.shape[0] // 4
        self.piece = self.rows // split
        self.copies = {}

    def send(self, kind, c):
        mask = (2, 1, 1)[kind]
        block = flip(self.index, 2) if kind == 2 else self.index
        rows = span(block * self.rows + c * self.piece, self.piece)
        slot = kind * self.split + c
        copy = pltpu.make_async_remote_copy(
            src_ref=self.whole.at[rows],
            dst_ref=self.whole.at[rows],
            send_sem=self.send_sems.at[slot],
            recv_sem=self.recv_sems.at[slot],
            device_id={"tensor": flip(self.index, mask)},
            device_id_type=MESH,
        )
        copy.start()
        self.copies[kind, c] = copy

    def start(self, c):
        self.send(0, c)
        self.send(1, c)

    def forward(self, c):
        self.copies[0, c].wait_recv()
        self.send(2, c)

    def near(self, c):
        self.copies[1, c].wait_recv()

    def finish(self, c):
        self.copies[2, c].wait_recv()

    def close(self):
        for copy in self.copies.values():
            copy.wait_send()


TENSOR_PEERS = (("tensor", 0), ("tensor", 1))
SPLIT = 4


def middle_kernel(
    o_ref,
    w_ref,
    gain_ref,
    tokens_hbm,
    gm_hbm,
    gate_hbm,
    up_hbm,
    down_hbm,
    h_ref,
    m_hbm,
    hid_hbm,
    dgate_hbm,
    dup_hbm,
    feed_hbm,
    dm_hbm,
    part,
    landing,
    m_buf,
    x_buf,
    gm_buf,
    gate_w,
    up_w,
    down_w,
    hid_buf,
    dgate_buf,
    dup_buf,
    rs_send,
    rs_recv,
    ag_send,
    ag_recv,
    load_sems,
    leave_sems,
    feed_buf,
):
    index = lax.axis_index("tensor")
    rows = o_ref.shape[0] // 4
    loads = [
        pltpu.make_async_copy(source, target, load_sems.at[i])
        for i, (source, target) in enumerate(
            (
                (tokens_hbm.at[span(index * rows, rows)], x_buf),
                (gate_hbm, gate_w),
                (up_hbm, up_w),
                (gm_hbm, gm_buf),
                (down_hbm, down_w),
            )
        )
    ]
    for load in loads:
        load.start()
    greet(TENSOR_PEERS)
    reduce = Reduce(part, landing, rs_send, rs_recv, "tensor", (0, 1), SPLIT)
    gather = Gather(m_buf, ag_send, ag_recv, SPLIT)
    leaving = []

    def leave(buffer, target, half):
        there = span(half * 2 * rows, 2 * rows)
        copy = pltpu.make_async_copy(
            buffer.at[there], target.at[there], leave_sems.at[len(leaving)]
        )
        copy.start()
        leaving.append(copy)

    def product(place):
        block = span(flip(index, place) * rows, rows)
        columns = 512

        def tile(i, carry):
            cols = pl.ds(pl.multiple_of(i * columns, columns), columns)
            part[block, cols] = nt(o_ref[block], w_ref[cols]).astype(jnp.bfloat16)
            return carry

        lax.fori_loop(0, part.shape[1] // columns, tile, 0)

    def normed(start, size, total):
        own = span(start, size)
        hidden = x_buf[own].astype(jnp.float32) + total
        h_ref[own] = hidden
        inverse = lax.rsqrt(jnp.mean(hidden * hidden, axis=-1, keepdims=True) + epsilon)
        m_buf[span(index * rows + start, size)] = (hidden * inverse * gain_ref[...]).astype(
            jnp.bfloat16
        )

    def hidden_part(half, first, last):
        there = span(half * 2 * rows, 2 * rows)
        columns = 256

        def tile(i, carry):
            cols = pl.ds(pl.multiple_of(i * columns, columns), columns)
            gate = nn(m_buf[there], gate_w[:, cols])
            upward = nn(m_buf[there], up_w[:, cols])
            grad = nn(gm_buf[there], down_w[:, cols])
            sigmoid = 1.0 / (1.0 + jnp.exp(-gate))
            activated = gate * sigmoid
            hid_buf[there, cols] = (activated * upward).astype(jnp.bfloat16)
            dgate_buf[there, cols] = (
                grad * upward * sigmoid * (1.0 + gate * (1.0 - sigmoid))
            ).astype(jnp.bfloat16)
            dup_buf[there, cols] = (grad * activated).astype(jnp.bfloat16)
            return carry

        lax.fori_loop(first, last, tile, 0)

    def feed_part(half):
        there = span(half * 2 * rows, 2 * rows)

        def tile(i, carry):
            cols = pl.ds(pl.multiple_of(i * 512, 512), 512)
            feed_buf[there, cols] = nt(hid_buf[there], down_w[cols]).astype(jnp.bfloat16)
            return carry

        lax.fori_loop(0, feed_buf.shape[1] // 512, tile, 0)

    def dm_part(half):
        there = span(half * 2 * rows, 2 * rows)

        def tile(i, carry):
            cols = pl.ds(pl.multiple_of(i * 512, 512), 512)
            total = nt(dgate_buf[there], gate_w[cols]) + nt(dup_buf[there], up_w[cols])
            part[there, cols] = total.astype(jnp.bfloat16)
            return carry

        lax.fori_loop(0, part.shape[1] // 512, tile, 0)

    product(3)
    for c in range(SPLIT):
        reduce.start(0, 0, c)
    product(2)
    for c in range(SPLIT):
        reduce.arrive(0, 0, c)
    product(1)
    for c in range(SPLIT):
        reduce.start(0, 1, c)
    product(0)
    for c in range(SPLIT):
        reduce.arrive(0, 1, c)
    loads[0].wait()
    for c in range(SPLIT):
        reduce.arrive(1, 0, c, normed)
        gather.start(c)
    near = lax.div(index, 2)
    far = 1 - near
    for load in loads[1:]:
        load.wait()
    for c in range(SPLIT):
        gather.near(c)
    reduce.close()
    tiles = hid_buf.shape[1] // 256
    hidden_part(near, 0, tiles // 2)
    gather.forward(0)
    hidden_part(near, tiles // 2, tiles)
    gather.forward(1)
    leave(hid_buf, hid_hbm, near)
    leave(dgate_buf, dgate_hbm, near)
    leave(dup_buf, dup_hbm, near)
    leave(m_buf, m_hbm, near)
    feed_part(near)
    leave(feed_buf, feed_hbm, near)
    gather.forward(2)
    dm_part(near)
    leave(part, dm_hbm, near)
    for c in range(3, SPLIT):
        gather.forward(c)
    for c in range(SPLIT):
        gather.finish(c)
    leave(m_buf, m_hbm, far)
    hidden_part(far, 0, tiles)
    leave(hid_buf, hid_hbm, far)
    leave(dgate_buf, dgate_hbm, far)
    leave(dup_buf, dup_hbm, far)
    feed_part(far)
    leave(feed_buf, feed_hbm, far)
    dm_part(far)
    leave(part, dm_hbm, far)
    for copy in leaving:
        copy.wait()
    gather.close()


def vmem_specs(count):
    return [pl.BlockSpec(memory_space=pltpu.VMEM)] * count


def dma_sems(count):
    return [pltpu.SemaphoreType.DMA((count,)), pltpu.SemaphoreType.DMA((count,))]


def middle_call(
    attended, mixing_weight, second_gain, tokens, outer_low, gate_weight, up_weight, down_weight
):
    slots, width = tokens.shape
    rows = slots // 4
    columns = gate_weight.shape[1]
    count = Reduce.slots(4, SPLIT)

    def low(*shape):
        return pltpu.VMEM(shape, jnp.bfloat16)

    def result(size):
        return jax.ShapeDtypeStruct((slots, size), jnp.bfloat16)

    return pl.pallas_call(
        middle_kernel,
        out_shape=(
            jax.ShapeDtypeStruct((rows, width), jnp.float32),
            result(width),
            result(columns),
            result(columns),
            result(columns),
            result(width),
            result(width),
        ),
        in_specs=vmem_specs(3) + [pl.BlockSpec(memory_space=pl.ANY)] * 5,
        out_specs=tuple(vmem_specs(1) + [pl.BlockSpec(memory_space=pl.ANY)] * 6),
        scratch_shapes=[
            low(slots, width),
            low(count, rows // SPLIT, width),
            low(slots, width),
            low(rows, width),
            low(slots, width),
            low(width, columns),
            low(width, columns),
            low(width, columns),
            low(slots, columns),
            low(slots, columns),
            low(slots, columns),
            *dma_sems(count),
            *dma_sems(3 * SPLIT),
            pltpu.SemaphoreType.DMA((5,)),
            pltpu.SemaphoreType.DMA((12,)),
            low(slots, width),
        ],
        compiler_params=pltpu.CompilerParams(
            collective_id=0, has_side_effects=True, vmem_limit_bytes=67043328
        ),
        name="middle",
    )(
        attended,
        mixing_weight,
        second_gain.reshape(1, -1),
        tokens,
        outer_low,
        gate_weight,
        up_weight,
        down_weight,
    )


BLOCK = 256
TILE = 384


def head(index):
    return pl.ds(index * HD, HD)


def allowed_keys(begin_row, query_start, key_count, query_count):
    keys = lax.broadcasted_iota(jnp.int32, (key_count, query_count), 0)
    queries = query_start + lax.broadcasted_iota(jnp.int32, (key_count, query_count), 1)
    return (keys >= begin_row) & (keys <= queries)


def rope_tables(slots):
    half = HD // 2
    frequency = rope_base ** (-2.0 * np.arange(half) / HD)

    def table(places):
        angles = places[:, None] * frequency[None, :]
        return np.concatenate([np.cos(angles), np.sin(angles)], axis=1).astype(np.float32)

    return (
        jnp.asarray(table(np.arange(BLOCK))),
        jnp.asarray(table(np.arange(max(8, slots // BLOCK)) * BLOCK)),
    )


def block_angles(base_ref, step_ref, block):
    half = HD // 2
    low_cos, low_sin = base_ref[:, pl.ds(0, half)], base_ref[:, pl.ds(half, half)]
    high = step_ref[pl.ds(block, 1)]
    high_cos, high_sin = high[:, :half], high[:, half:]
    return (low_cos * high_cos - low_sin * high_sin, low_sin * high_cos + low_cos * high_sin)


def turn(values, cosine, sine):
    half = HD // 2
    first, second = values[:, :half], values[:, half:]
    return jnp.concatenate([first * cosine - second * sine, second * cosine + first * sine], axis=1)


def first_kernel(
    blocks,
    lengths_ref,
    owners_ref,
    x_ref,
    cot_ref,
    gain_ref,
    wq_ref,
    wk_ref,
    wv_ref,
    base_ref,
    step_ref,
    a_ref,
    gm_ref,
    q_ref,
    kv_ref,
    o_ref,
    lse_ref,
    begin_ref,
    used_ref,
    kept,
    turned,
    o_heads,
):
    block = pl.program_id(0)
    index = lax.axis_index("dp")
    slots = block * BLOCK + lax.broadcasted_iota(jnp.int32, (1, BLOCK), 1)

    def sequence(s, carry):
        total, begin = carry
        length = jnp.where(owners_ref[s] == index, lengths_ref[s], 0)
        begin = jnp.where((slots >= total) & (slots < total + length), total, begin)
        return total + length, begin

    used, begin = lax.fori_loop(0, lengths_ref.shape[0], sequence, (jnp.int32(0), slots))
    begin_ref[...] = begin
    used_ref[0] = used
    size = 64

    def rows_in(i, carry):
        rows = span(i * size, size)
        values = x_ref[rows].astype(jnp.float32)
        inverse = lax.rsqrt(jnp.mean(values * values, axis=-1, keepdims=True) + epsilon)
        a_ref[rows] = (values * inverse * gain_ref[...]).astype(jnp.bfloat16)
        places = block * BLOCK + i * size + lax.broadcasted_iota(jnp.int32, (size, 1), 0)
        live = (places < used).astype(jnp.float32)
        gm_ref[rows] = (cot_ref[rows].astype(jnp.float32) * live).astype(jnp.bfloat16)
        return carry

    lax.fori_loop(0, BLOCK // size, rows_in, 0)
    cosine, sine = block_angles(base_ref, step_ref, block)
    normed = a_ref[...]
    queries = nn(normed, wq_ref[...])
    query_heads, key_heads = queries.shape[1] // HD, wk_ref.shape[0] // HD
    for h in range(query_heads):
        piece = queries[:, h * HD : (h + 1) * HD]
        q_ref[h] = turn(piece, cosine, sine).astype(jnp.bfloat16)
    keys = nt(normed, wk_ref[...])
    here = span(block * BLOCK, BLOCK)
    for h in range(key_heads):
        piece = turn(keys[:, h * HD : (h + 1) * HD], cosine, sine).astype(jnp.bfloat16)
        kv_ref[h] = piece
        kept[h, here] = piece
    values = nt(normed, wv_ref[...]).astype(jnp.bfloat16)
    for h in range(key_heads):
        kv_ref[key_heads + h] = values[:, h * HD : (h + 1) * HD]
    scaling = HD ** (-0.5)
    groups = query_heads // key_heads

    def attend(now):
        stop = (now + 1) * BLOCK
        for h in range(key_heads):
            turned[h, :, pl.ds(now * BLOCK, BLOCK)] = kv_ref[key_heads + h].T
        allowed = allowed_keys(begin, now * BLOCK, stop, BLOCK)

        def one_head(h, carry):
            group = lax.div(h, groups)
            scores = nt(kept[group, pl.ds(0, stop)], q_ref[h]) * scaling
            scores = jnp.where(allowed, scores, -jnp.inf)
            highest = jnp.max(scores, axis=0, keepdims=True)
            exponent = jnp.exp(scores - highest)
            total = jnp.sum(exponent, axis=0, keepdims=True)
            weights = (exponent * (1.0 / total)).astype(jnp.bfloat16)
            mixed = nn(turned[group, :, pl.ds(0, stop)], weights)
            o_heads[h] = mixed.T.astype(jnp.bfloat16)
            lse_ref[pl.ds(h, 1)] = highest + jnp.log(total)
            return carry

        lax.fori_loop(0, query_heads, one_head, 0)

    for now in range(blocks):
        pl.when(block == now)(lambda now=now: attend(now))
    for h in range(query_heads):
        o_ref[:, head(h)] = o_heads[h]


def first_call(
    tokens, lengths, owners, first_gain, query_weight, key_weight, value_weight, cotangent, tables
):
    slots, width = tokens.shape
    blocks = slots // BLOCK
    columns, pairs = query_weight.shape[1], 2 * key_weight.shape[0] // HD
    heads = columns // HD

    def kernel(*refs):
        first_kernel(blocks, *refs)

    def rows_of(size):
        return pl.BlockSpec((BLOCK, size), lambda i: (i, 0))

    def whole(array):
        return pl.BlockSpec(array.shape, lambda i: (0, 0), pipeline_mode=pl.Buffered(1))

    gain = first_gain.reshape(1, -1)
    scalars = pl.BlockSpec(memory_space=pltpu.SMEM)
    return pl.pallas_call(
        kernel,
        grid=(blocks,),
        out_shape=(
            jax.ShapeDtypeStruct((slots, width), jnp.bfloat16),
            jax.ShapeDtypeStruct((slots, width), jnp.bfloat16),
            jax.ShapeDtypeStruct((heads, slots, HD), jnp.bfloat16),
            jax.ShapeDtypeStruct((pairs, slots, HD), jnp.bfloat16),
            jax.ShapeDtypeStruct((slots, columns), jnp.bfloat16),
            jax.ShapeDtypeStruct((heads, slots), jnp.float32),
            jax.ShapeDtypeStruct((1, slots), jnp.int32),
            jax.ShapeDtypeStruct((1,), jnp.int32),
        ),
        in_specs=[
            scalars,
            scalars,
            rows_of(width),
            rows_of(width),
            whole(gain),
            whole(query_weight),
            whole(key_weight),
            whole(value_weight),
            whole(tables[0]),
            whole(tables[1]),
        ],
        out_specs=(
            rows_of(width),
            rows_of(width),
            pl.BlockSpec((heads, BLOCK, HD), lambda i: (0, i, 0)),
            pl.BlockSpec((pairs, BLOCK, HD), lambda i: (0, i, 0)),
            rows_of(columns),
            pl.BlockSpec((heads, BLOCK), lambda i: (0, i)),
            pl.BlockSpec((1, BLOCK), lambda i: (0, i)),
            scalars,
        ),
        scratch_shapes=[
            pltpu.VMEM((pairs // 2, slots, HD), jnp.bfloat16),
            pltpu.VMEM((pairs // 2, HD, slots), jnp.bfloat16),
            pltpu.VMEM((heads, BLOCK, HD), jnp.bfloat16),
        ],
        compiler_params=pltpu.CompilerParams(vmem_limit_bytes=67043328),
        name="first",
    )(
        lengths,
        owners,
        tokens,
        cotangent,
        gain,
        query_weight,
        key_weight,
        value_weight,
        *tables,
    )


def last_kernel(group_columns, *refs):
    sources, targets, buffers = refs[:8], refs[8:17], refs[17:28]
    in_sems, out_sems = refs[28:]
    out, token, down, gate, up, mix, one, two = buffers[:8]
    turned = buffers[8:]
    coming = [
        pltpu.make_async_copy(source, buffer, in_sems.at[i])
        for i, (source, buffer) in enumerate(zip(sources, buffers[:8]))
    ]
    for copy in coming:
        copy.start()
    leaving = []

    def leave(buffer):
        i = len(leaving)
        copy = pltpu.make_async_copy(buffer, targets[i], out_sems.at[i])
        copy.start()
        leaving.append(copy)

    for i in (0, 1, 2, 3, 4, 5):
        coming[i].wait()
        leave(buffers[i])
    start = 0
    coming[6].wait()
    coming[7].wait()
    for buffer in turned:
        each = buffer.shape[1] // 2
        buffer[:, pl.ds(0, each)] = one[:, pl.ds(start, each)]
        buffer[:, pl.ds(each, each)] = two[:, pl.ds(start, each)]
        start += each
        leave(buffer)
    for copy in leaving:
        copy.wait()


def last_call(arrays, query_columns, key_columns):
    rows = arrays[6].shape[0]
    shapes = [jax.ShapeDtypeStruct(array.shape, array.dtype) for array in arrays[:6]]
    shapes += [
        jax.ShapeDtypeStruct((rows, size), jnp.float32)
        for size in (query_columns, key_columns, key_columns)
    ]

    def kernel(*refs):
        last_kernel(TILE, *refs)

    buffers = [pltpu.VMEM(array.shape, array.dtype) for array in arrays]
    buffers += [pltpu.VMEM(shape.shape, shape.dtype) for shape in shapes[6:]]
    return pl.pallas_call(
        kernel,
        out_shape=tuple(shapes),
        in_specs=[pl.BlockSpec(memory_space=pl.ANY)] * 8,
        out_specs=tuple([pl.BlockSpec(memory_space=pl.ANY)] * 9),
        scratch_shapes=[
            *buffers,
            pltpu.SemaphoreType.DMA((8,)),
            pltpu.SemaphoreType.DMA((9,)),
        ],
        compiler_params=pltpu.CompilerParams(vmem_limit_bytes=67043328),
        name="last",
    )(*arrays)


def lanes(index):
    return pl.ds(pl.multiple_of(index * 128, 128), HD)


def attention_back(q_ref, kv_ref, grads, begin_ref, lse_ref, turned, sums, heads, group, start, leave):
    scaling = HD ** (-0.5)
    key_sum, value_sum = sums
    key_heads = kv_ref.shape[0] // 2
    stop = start + BLOCK
    rows = pl.ds(start, BLOCK)
    seen = pl.ds(0, stop)
    if stop == q_ref.shape[1]:
        key_sum[...] = jnp.zeros_like(key_sum)
        value_sum[...] = jnp.zeros_like(value_sum)
    allowed = allowed_keys(begin_ref[:, rows], start, stop, BLOCK)

    def one_head(h, carry):
        query = q_ref[h, rows]
        grad = grads[rows, lanes(h)]
        scores = nt(kv_ref[group, seen], query) * scaling
        weights = jnp.where(allowed, jnp.exp(scores - lse_ref[pl.ds(h, 1), rows]), 0.0)
        weights_grad = nt(kv_ref[key_heads + group, seen], grad)
        inner = jnp.sum(weights * weights_grad, axis=0, keepdims=True)
        scores_grad = (weights * (weights_grad - inner)).astype(jnp.bfloat16)
        value_sum[seen] += nn(weights.astype(jnp.bfloat16), grad)
        key_sum[seen] += nn(scores_grad, query)
        leave(h, rows, nn(turned[:, :stop], scores_grad).T * scaling)
        return carry

    lax.fori_loop(heads[0], heads[1], one_head, 0)


P_START = "start"
P_TILE = "tile"
P_ARRIVE = "arrive"
P_FORWARD = "forward"
P_FINISH = "finish"
P_BACK = "back"
P_ATTENTION = "attention"
P_KEYS = "keys"
P_PRODUCT = "product"
P_SEND = "send"
P_ADD = "add"
P_DM = "dm"
P_FEED = "feed"
P_DA = "da"
P_DOWN = "down"
P_GATE = "gate"
P_UP = "up"
P_MIX = "mix"
P_ONE = "one"
P_TWO = "two"

PLAN = (
    (P_TILE, P_GATE, 3),
    (P_TILE, P_DOWN, 3),
    (P_START, P_DM),
    (P_TILE, P_GATE, 1),
    (P_ARRIVE, P_DM, 0, 0, 2),
    (P_ARRIVE, P_DM, 0, 1, 1),
    (P_ARRIVE, P_DM, 0, 1, 0),
    (P_ARRIVE, P_DM, 0, 0, 0),
    (P_TILE, P_DOWN, 1),
    (P_TILE, P_GATE, 2),
    (P_ARRIVE, P_DM, 0, 0, 1),
    (P_TILE, P_DOWN, 2),
    (P_ARRIVE, P_DM, 0, 1, 3),
    (P_ARRIVE, P_DM, 1, 0, 1),
    (P_ARRIVE, P_DM, 0, 1, 2),
    (P_ARRIVE, P_DM, 0, 0, 3),
    (P_ARRIVE, P_GATE, 0, 0, 0),
    (P_TILE, P_GATE, 0),
    (P_ARRIVE, P_GATE, 0, 1, 0),
    (P_FORWARD, 1),
    (P_TILE, P_DOWN, 0),
    (P_ARRIVE, P_DOWN, 0, 2, 0),
    (P_ARRIVE, P_GATE, 0, 2, 0),
    (P_ARRIVE, P_DOWN, 0, 0, 0),
    (P_ARRIVE, P_DM, 1, 0, 2),
    (P_TILE, P_UP, 3),
    (P_ARRIVE, P_DM, 1, 0, 0),
    (P_TILE, P_UP, 1),
    (P_FINISH, 1),
    (P_TILE, P_UP, 2),
    (P_ARRIVE, P_DM, 1, 0, 3),
    (P_FORWARD, 0),
    (P_TILE, P_UP, 0),
    (P_ARRIVE, P_DOWN, 0, 1, 0),
    (P_FORWARD, 2),
    (P_ARRIVE, P_GATE, 0, 3, 0),
    (P_FINISH, 0),
    (P_FORWARD, 3),
    (P_FINISH, 3),
    (P_ARRIVE, P_DOWN, 1, 0, 0),
    (P_FINISH, 2),
    (P_START, P_FEED),
    (P_ARRIVE, P_FEED, 0, 0, 0),
    (P_TILE, P_MIX, 3),
    (P_ARRIVE, P_FEED, 0, 0, 1),
    (P_ARRIVE, P_FEED, 0, 0, 2),
    (P_TILE, P_MIX, 1),
    (P_TILE, P_MIX, 2),
    (P_TILE, P_MIX, 0),
    (P_ARRIVE, P_FEED, 0, 1, 1),
    (P_ARRIVE, P_FEED, 0, 0, 3),
    (P_ARRIVE, P_UP, 0, 0, 0),
    (P_ARRIVE, P_GATE, 1, 0, 0),
    (P_BACK,),
    (P_ARRIVE, P_FEED, 1, 0, 1),
    (P_ATTENTION, 0, 3),
    (P_ARRIVE, P_UP, 0, 1, 0),
    (P_ARRIVE, P_FEED, 0, 1, 0),
    (P_ARRIVE, P_DOWN, 0, 3, 0),
    (P_ATTENTION, 0, 2),
    (P_ATTENTION, 0, 1),
    (P_ATTENTION, 0, 0),
    (P_KEYS, 0),
    (P_ARRIVE, P_FEED, 1, 0, 0),
    (P_TILE, P_ONE, 3),
    (P_TILE, P_ONE, 1),
    (P_ARRIVE, P_GATE, 1, 1, 0),
    (P_TILE, P_ONE, 2),
    (P_TILE, P_ONE, 0),
    (P_ARRIVE, P_FEED, 0, 1, 2),
    (P_ARRIVE, P_FEED, 1, 0, 2),
    (P_ATTENTION, 1, 3),
    (P_ATTENTION, 1, 2),
    (P_ARRIVE, P_FEED, 0, 1, 3),
    (P_ARRIVE, P_UP, 0, 2, 0),
    (P_ARRIVE, P_FEED, 1, 0, 3),
    (P_ATTENTION, 1, 1),
    (P_ATTENTION, 1, 0),
    (P_ARRIVE, P_MIX, 0, 0, 0),
    (P_ARRIVE, P_UP, 1, 0, 0),
    (P_ARRIVE, P_GATE, 2, 0, 0),
    (P_KEYS, 1),
    (P_ARRIVE, P_DOWN, 1, 1, 0),
    (P_ARRIVE, P_DOWN, 2, 0, 0),
    (P_TILE, P_TWO, 3),
    (P_TILE, P_TWO, 1),
    (P_TILE, P_TWO, 2),
    (P_TILE, P_TWO, 0),
    (P_PRODUCT, 3),
    (P_PRODUCT, 1),
    (P_PRODUCT, 2),
    (P_ARRIVE, P_DA, 0, 0, 1),
    (P_PRODUCT, 0),
    (P_ARRIVE, P_DA, 0, 1, 1),
    (P_ARRIVE, P_DA, 0, 0, 0),
    (P_ARRIVE, P_MIX, 0, 1, 0),
    (P_ARRIVE, P_DA, 0, 0, 3),
    (P_ARRIVE, P_UP, 0, 3, 0),
    (P_ARRIVE, P_DA, 0, 1, 0),
    (P_ARRIVE, P_ONE, 0, 0, 0),
    (P_ARRIVE, P_DA, 0, 1, 2),
    (P_ARRIVE, P_MIX, 0, 2, 0),
    (P_ARRIVE, P_DA, 1, 0, 0),
    (P_ARRIVE, P_MIX, 0, 3, 0),
    (P_ARRIVE, P_MIX, 1, 0, 0),
    (P_ARRIVE, P_DA, 0, 0, 2),
    (P_ARRIVE, P_DA, 1, 0, 1),
    (P_ARRIVE, P_ONE, 0, 1, 0),
    (P_ARRIVE, P_ONE, 0, 2, 0),
    (P_ARRIVE, P_TWO, 0, 0, 0),
    (P_ARRIVE, P_MIX, 1, 1, 0),
    (P_ARRIVE, P_TWO, 0, 1, 0),
    (P_ARRIVE, P_DA, 1, 0, 2),
    (P_ARRIVE, P_UP, 1, 1, 0),
    (P_ARRIVE, P_DA, 0, 1, 3),
    (P_ARRIVE, P_DA, 1, 0, 3),
    (P_SEND, 0),
    (P_ARRIVE, P_TWO, 0, 2, 0),
    (P_ADD, 0),
    (P_ARRIVE, P_ONE, 1, 0, 0),
    (P_ARRIVE, P_UP, 2, 0, 0),
    (P_SEND, 1),
    (P_ADD, 1),
    (P_SEND, 2),
    (P_ADD, 2),
    (P_SEND, 3),
    (P_ARRIVE, P_TWO, 1, 0, 0),
    (P_ADD, 3),
    (P_ARRIVE, P_ONE, 0, 3, 0),
    (P_ARRIVE, P_MIX, 2, 0, 0),
    (P_ARRIVE, P_TWO, 0, 3, 0),
    (P_ARRIVE, P_TWO, 1, 1, 0),
    (P_ARRIVE, P_ONE, 1, 1, 0),
    (P_ARRIVE, P_ONE, 2, 0, 0),
    (P_SEND, 4),
    (P_ARRIVE, P_TWO, 2, 0, 0),
    (P_ADD, 4),
)


def plan_of(count, orders, reduces):
    if count == 8:
        return PLAN
    tiles = (3, 1, 2, 0)

    def units(name, step):
        return [(P_ARRIVE, name, step, j, c) for j, c in reduces[name].units(step)]

    plan = [(P_START, P_DM)]
    plan += [(P_TILE, name, which) for name in (P_DOWN, P_GATE, P_UP) for which in tiles]
    plan += units(P_DM, 0) + units(P_DM, 1)
    plan += [(P_FORWARD, c) for c in range(SPLIT)] + [(P_FINISH, c) for c in range(SPLIT)]
    plan += [(P_START, P_FEED)] + [(P_TILE, P_MIX, which) for which in tiles] + [(P_BACK,)]
    for group in range(2):
        plan += [(P_ATTENTION, group, block) for block in (3, 2, 1, 0)]
        plan += [(P_KEYS, group)]
        plan += [(P_TILE, (P_ONE, P_TWO)[group], which) for which in tiles]
    plan += units(P_FEED, 0) + units(P_FEED, 1)
    plan += [(P_PRODUCT, place) for place in (3, 1, 2, 0)] + units(P_DA, 0) + units(P_DA, 1)
    names = (P_DOWN, P_GATE, P_UP, P_MIX, P_ONE, P_TWO)
    for step in range(len(orders[0])):
        for name in names:
            plan += units(name, step)
    for i in range(2 + len(orders[0])):
        plan += [(P_SEND, i), (P_ADD, i)]
    return plan


def back_kernel(
    dp_order,
    z_order,
    dm_hbm,
    feed_hbm,
    m_hbm,
    gm_hbm,
    hid_hbm,
    dgate_hbm,
    dup_hbm,
    a_hbm,
    tokens_hbm,
    used_ref,
    h_ref,
    gain1_ref,
    gain2_ref,
    mixing_ref,
    query_ref,
    key_ref,
    value_ref,
    o_ref,
    q_ref,
    kv_ref,
    begin_ref,
    lse_ref,
    base_ref,
    step_ref,
    out_ref,
    token_ref,
    gains_ref,
    down_ref,
    gate_ref,
    up_ref,
    mix_ref,
    one_ref,
    two_ref,
    *scratch,
):
    (
        wide,
        m_buf,
        hid_buf,
        dgate_buf,
        rs_part,
        rs_land,
        ga_buf,
        dh_buf,
        key_sum,
        value_sum,
        gains_land,
        cot_ref,
        result,
        *scratch,
    ) = scratch
    parts, lands, sems = scratch[:6], scratch[6:12], scratch[12:]
    stage, stage_sem, out_sem, load_sems, credit, *sems = sems
    index = lax.axis_index("tensor")
    dp_index = lax.axis_index("dp")
    count = 1 << len(dp_order)

    own_rows = span(index * h_ref.shape[0], h_ref.shape[0])
    loads = [
        pltpu.make_async_copy(source, target, load_sems.at[i])
        for i, (source, target) in enumerate(
            (
                (dm_hbm, rs_part),
                (gm_hbm, wide),
                (hid_hbm, hid_buf),
                (m_hbm, m_buf),
                (dgate_hbm, dgate_buf),
                (dup_hbm, hid_buf),
                (feed_hbm, rs_part),
                (a_hbm, wide),
                (gm_hbm.at[own_rows], cot_ref),
                (tokens_hbm.at[own_rows], cot_ref),
            )
        )
    ]
    for i in (3, 4, 1, 2, 0, 8):
        loads[i].start()
    greet(TENSOR_PEERS + tuple(("dp", bit) for bit in dp_order))

    def share_reduce(first_sem):
        return Reduce(rs_part, rs_land, sems[first_sem], sems[first_sem + 1], "tensor", (0, 1), SPLIT)

    dm, feed, da = share_reduce(0), share_reduce(2), share_reduce(4)
    gather = Gather(ga_buf, sems[6], sems[7], SPLIT)
    orders = (z_order, dp_order, dp_order, dp_order, dp_order, dp_order)
    down, gate, up, mix, one, two = (
        Reduce(parts[i], lands[i], sems[8 + 2 * i], sems[9 + 2 * i], "dp", orders[i])
        for i in range(6)
    )
    gains_send, gains_recv = sems[20], sems[21]
    gains_ref[...] = jnp.zeros_like(gains_ref)

    def finish_out(start, size, total):
        own = span(start, size)
        places = index * h_ref.shape[0] + start + lax.broadcasted_iota(jnp.int32, (size, 1), 0)
        live = (places < used_ref[0]).astype(jnp.float32)
        result[own] = ((h_ref[own] + total) * live).astype(jnp.bfloat16)

    def finish_dm(start, size, total):
        own = span(start, size)
        hidden = h_ref[own]
        inverse = lax.rsqrt(jnp.mean(hidden * hidden, axis=-1, keepdims=True) + epsilon)
        scaled = total * gain2_ref[...]
        inner = jnp.mean(scaled * hidden, axis=-1, keepdims=True)
        grad = (
            cot_ref[own].astype(jnp.float32)
            + inverse * scaled
            - hidden * (inverse * inverse * inverse) * inner
        )
        dh_buf[own] = grad
        ga_buf[span(index * dh_buf.shape[0] + start, size)] = grad.astype(jnp.bfloat16)
        gains_ref[pl.ds(1, 1)] += jnp.sum(total * hidden * inverse, axis=0, keepdims=True)

    def finish_da(start, size, total):
        own = span(start, size)
        values = cot_ref[own].astype(jnp.float32)
        inverse = lax.rsqrt(jnp.mean(values * values, axis=-1, keepdims=True) + epsilon)
        scaled = total * gain1_ref[...]
        inner = jnp.mean(scaled * values, axis=-1, keepdims=True)
        grad = dh_buf[own] + inverse * scaled - values * (inverse * inverse * inverse) * inner
        result[own] = grad.astype(jnp.bfloat16)
        gains_ref[pl.ds(0, 1)] += jnp.sum(total * values * inverse, axis=0, keepdims=True)

    out_copy = pltpu.make_async_copy(result, out_ref, out_sem.at[0])
    token_copy = pltpu.make_async_copy(result, token_ref, out_sem.at[1])
    flying = []

    def settle():
        for copy in flying:
            copy.wait()
        flying.clear()

    def finish_grad(reduce, target):
        settle()
        columns = pl.ds(0, reduce.part.shape[1])

        def store(start, size, total):
            stage[span(start, size), columns] = total

        reduce.arrive_all(last, store)
        copy = pltpu.make_async_copy(stage.at[:, columns], target, stage_sem)
        copy.start()
        flying.append(copy)

    def grad_tile(left, right, columns, reduce, which):
        blocks = TILE // reduce.rows
        tile = flip(lax.div(dp_index, blocks), which) * TILE
        cols = pl.ds(pl.multiple_of(tile, 128), TILE)
        width = columns.stop - columns.start
        step = min(width, 512)

        def some(i, carry):
            there = pl.ds(pl.multiple_of(i * step, 128), step)
            here = pl.ds(pl.multiple_of(columns.start + i * step, 128), step)
            reduce.part[span(tile, TILE), there] = tn(left[:, cols], right[:, here]).astype(
                jnp.bfloat16
            )
            return carry

        lax.fori_loop(0, width // step, some, 0)
        kept, _ = reduce.lists[0]
        for j, kept_place in enumerate(kept):
            if (kept_place | (1 << reduce.order[0])) // blocks == which:
                reduce.start(0, j)

    slots, hidden_columns = hid_buf.shape
    query_heads = q_ref.shape[0]
    query_columns, key_columns = query_heads * HD, kv_ref.shape[0] * HD // 2
    queries_each = query_columns // key_columns
    scaling = HD ** (-0.5)
    last = len(dp_order) - 1
    reduces = {
        "dm": dm,
        "feed": feed,
        "da": da,
        "down": down,
        "gate": gate,
        "up": up,
        "mix": mix,
        "one": one,
        "two": two,
    }
    targets = {
        "down": down_ref,
        "gate": gate_ref,
        "up": up_ref,
        "mix": mix_ref,
        "one": one_ref,
        "two": two_ref,
    }
    sources = {
        "down": (wide, hid_buf, slice(0, hidden_columns)),
        "gate": (m_buf, dgate_buf, slice(0, hidden_columns)),
        "up": (m_buf, hid_buf, slice(0, hidden_columns)),
        "mix": (ga_buf, o_ref, slice(0, query_columns)),
        "one": (wide, dgate_buf, slice(0, TILE)),
        "two": (wide, dgate_buf, slice(TILE, 2 * TILE)),
    }
    before = {
        ("down", 3): (1, 2),
        ("gate", 3): (3, 4),
        ("up", 3): (5,),
        ("one", 3): (7,),
    }
    peers = TENSOR_PEERS + tuple(("dp", bit) for bit in dp_order)
    gains = []
    turned = {}

    def turned_back(values, block):
        cosine, sine = block_angles(base_ref, step_ref, block)
        return turn(values, cosine, -sine).astype(jnp.bfloat16)

    def keep(rows, values, grouped, plain):
        dgate_buf[rows, pl.ds(grouped, HD)] = values
        hid_buf[rows, pl.ds(plain, HD)] = values

    def do_start(name):
        if name == "dm":
            loads[0].wait()
            loads[8].wait()
        else:
            dm.close()
            loads[9].start()
            loads[6].start()
            loads[6].wait()
        reduces[name].start_all()

    def do_tile(name, which):
        for i in before.get((name, which), ()):
            loads[i].wait()
        left, right, columns = sources[name]
        grad_tile(left, right, columns, reduces[name], which)
        if (name, which) == ("down", 0):
            loads[5].start()
            loads[7].start()

    def do_arrive(name, step, j, c):
        reduce = reduces[name]
        if name in targets:
            if step == last:
                finish_grad(reduce, targets[name])
            else:
                reduce.arrive(step, j, c)
        elif step == 0:
            reduce.arrive(step, j, c)
        else:
            reduce.arrive(step, j, c, {"dm": finish_dm, "feed": finish_out, "da": finish_da}[name])
            if name == "dm":
                gather.start(c)
            if name == "feed" and c == SPLIT - 1:
                for mask in (1, 2):
                    pl.semaphore_signal(
                        credit,
                        inc=1,
                        device_id={"tensor": flip(index, mask)},
                        device_id_type=MESH,
                    )
                feed.close()
                out_copy.start()
            if name == "da" and c == SPLIT - 1:
                token_copy.start()

    def do_back():
        def some(i, carry):
            rows = span(i * BLOCK, BLOCK)
            grads = nn(ga_buf[rows], mixing_ref[...]).astype(jnp.bfloat16)
            for h in range(query_heads):
                m_buf[rows, lanes(h)] = grads[:, h * HD : (h + 1) * HD]
            return carry

        lax.fori_loop(0, slots // BLOCK, some, 0)

    def do_attention(group, block):
        if group not in turned:
            turned[group] = kv_ref[group].T

        def leave(h, rows, values):
            m_buf[rows, lanes(query_heads + h)] = turned_back(values, block)

        attention_back(
            q_ref,
            kv_ref,
            m_buf,
            begin_ref,
            lse_ref,
            turned[group],
            (key_sum, value_sum),
            (group * queries_each, (group + 1) * queries_each),
            group,
            block * BLOCK,
            leave,
        )

    def do_keys(group):
        grouped = group * TILE + queries_each * HD
        plain = query_columns + group * HD

        def some(i, carry):
            rows = span(i * BLOCK, BLOCK)
            for each in range(queries_each):
                h = group * queries_each + each
                keep(rows, m_buf[rows, lanes(query_heads + h)], group * TILE + each * HD, h * HD)
            keep(rows, turned_back(key_sum[rows] * scaling, i), grouped, plain)
            keep(rows, value_sum[rows].astype(jnp.bfloat16), grouped + HD, plain + key_columns)
            return carry

        lax.fori_loop(0, slots // BLOCK, some, 0)

    def do_product(place):
        if place == 3:
            loads[9].wait()
            out_copy.wait()
            pl.semaphore_wait(credit, 2)
        block = span(flip(index, place) * BLOCK, BLOCK)

        def some(i, carry):
            cols = pl.ds(pl.multiple_of(i * 512, 512), 512)
            total = nt(hid_buf[block, pl.ds(0, query_columns)], query_ref[cols])
            total += nn(hid_buf[block, pl.ds(query_columns, key_columns)], key_ref[:, cols])
            total += nn(
                hid_buf[block, pl.ds(query_columns + key_columns, key_columns)], value_ref[:, cols]
            )
            rs_part[block, cols] = total.astype(jnp.bfloat16)
            return carry

        lax.fori_loop(0, rs_part.shape[1] // 512, some, 0)
        if place in (3, 1):
            for c in range(SPLIT):
                da.start(0, (3, 1).index(place), c)

    def do_send_gains(i):
        axis, bit = peers[i]
        copy = pltpu.make_async_remote_copy(
            src_ref=gains_ref,
            dst_ref=gains_land.at[i],
            send_sem=gains_send.at[i],
            recv_sem=gains_recv.at[i],
            device_id={axis: flip(lax.axis_index(axis), 1 << bit)},
            device_id_type=MESH,
        )
        copy.start()
        gains.append(copy)

    def do_finish(c):
        gather.near(c)
        gather.finish(c)

    def do_add_gains(i):
        gains[i].wait()
        gains_ref[...] += gains_land[i]

    actions = {
        "start": do_start,
        "tile": do_tile,
        "arrive": do_arrive,
        "forward": gather.forward,
        "finish": do_finish,
        "back": do_back,
        "attention": do_attention,
        "keys": do_keys,
        "product": do_product,
        "send": do_send_gains,
        "add": do_add_gains,
    }
    for action, *rest in plan_of(count, orders, reduces):
        actions[action](*rest)
    settle()
    token_copy.wait()
    for item in (da, gather, down, gate, up, mix, one, two):
        item.close()


def back_call(
    dm_part,
    feed_part,
    second_in,
    outer_low,
    hidden,
    gate_low,
    upward_low,
    first_in,
    tokens,
    used,
    middle,
    first_gain,
    second_gain,
    mixing_weight,
    query_weight,
    key_weight,
    value_weight,
    attended,
    queries,
    pairs,
    begin,
    log_totals,
    tables,
):
    slots, width = dm_part.shape
    rows = slots // 4
    columns = hidden.shape[1]
    heads = attended.shape[1]
    count = lax.axis_size("dp")
    dp_order = bits_of(count)
    z_order = (dp_order[1], dp_order[0]) + dp_order[2:]
    block = width // count
    share = Reduce.slots(4, SPLIT)
    total = Reduce.slots(count)

    def kernel(*refs):
        back_kernel(dp_order, z_order, *refs)

    def grad(size):
        return jax.ShapeDtypeStruct((block, size), jnp.float32)

    def low(*shape):
        return pltpu.VMEM(shape, jnp.bfloat16)

    sizes = (columns, columns, columns, heads, TILE, TILE)
    hops = 2 + len(dp_order)
    return pl.pallas_call(
        kernel,
        out_shape=(
            jax.ShapeDtypeStruct((rows, width), jnp.bfloat16),
            jax.ShapeDtypeStruct((rows, width), jnp.bfloat16),
            jax.ShapeDtypeStruct((2, width), jnp.float32),
            *(grad(size) for size in sizes),
        ),
        in_specs=[pl.BlockSpec(memory_space=pl.ANY)] * 9
        + [pl.BlockSpec(memory_space=pltpu.SMEM)]
        + vmem_specs(14),
        out_specs=tuple(
            pl.BlockSpec(memory_space=pltpu.VMEM if i == 2 else pl.ANY) for i in range(9)
        ),
        scratch_shapes=[
            low(slots, width),
            low(slots, width),
            low(slots, columns),
            low(slots, columns),
            low(slots, width),
            low(share, rows // SPLIT, width),
            low(slots, width),
            pltpu.VMEM((rows, width), jnp.float32),
            pltpu.VMEM((slots, HD), jnp.float32),
            pltpu.VMEM((slots, HD), jnp.float32),
            pltpu.VMEM((hops, 2, width), jnp.float32),
            low(rows, width),
            low(rows, width),
            *(low(width, size) for size in sizes),
            *(low(total, block, size) for size in sizes),
            pltpu.VMEM((block, columns), jnp.float32),
            pltpu.SemaphoreType.DMA,
            pltpu.SemaphoreType.DMA((2,)),
            pltpu.SemaphoreType.DMA((10,)),
            pltpu.SemaphoreType.REGULAR,
            *dma_sems(share),
            *dma_sems(share),
            *dma_sems(share),
            *dma_sems(3 * SPLIT),
            *(sem for size in sizes for sem in dma_sems(total)),
            *dma_sems(hops),
        ],
        compiler_params=pltpu.CompilerParams(
            collective_id=1, has_side_effects=True, vmem_limit_bytes=67043328
        ),
        name="back",
    )(
        dm_part,
        feed_part,
        second_in,
        outer_low,
        hidden,
        gate_low,
        upward_low,
        first_in,
        tokens,
        used,
        middle,
        first_gain.reshape(1, -1),
        second_gain.reshape(1, -1),
        mixing_weight,
        query_weight,
        key_weight,
        value_weight,
        attended,
        queries,
        pairs,
        begin,
        log_totals,
        *tables,
    )


def on_device(
    tokens,
    lengths,
    owners,
    first_gain,
    query_weight,
    key_weight,
    value_weight,
    mixing_weight,
    second_gain,
    gate_weight,
    up_weight,
    down_weight,
    cotangent,
):
    tables = rope_tables(tokens.shape[0])
    key_turned, value_turned = key_weight.T, value_weight.T
    first_in, outer_low, queries, pairs, attended, log_totals, begin, used = first_call(
        tokens,
        lengths,
        owners,
        first_gain,
        query_weight,
        key_turned,
        value_turned,
        cotangent,
        tables,
    )
    middle, second_in, hidden, gate_low, upward_low, feed_part, second_part = middle_call(
        attended,
        mixing_weight,
        second_gain,
        tokens,
        outer_low,
        gate_weight,
        up_weight,
        down_weight,
    )
    layer_output, token_grad, gains, *grads = back_call(
        second_part,
        feed_part,
        second_in,
        outer_low,
        hidden,
        gate_low,
        upward_low,
        first_in,
        tokens,
        used,
        middle,
        first_gain,
        second_gain,
        mixing_weight,
        query_weight,
        key_turned,
        value_turned,
        attended,
        queries,
        pairs,
        begin,
        log_totals,
        tables,
    )
    (
        layer_output,
        token_grad,
        down_grad,
        gate_grad,
        up_grad,
        mixing_grad,
        query_grad,
        key_grad,
        value_grad,
    ) = last_call([layer_output, token_grad, *grads], query_weight.shape[1], key_weight.shape[1])
    return (
        layer_output,
        token_grad,
        gains[0],
        query_grad,
        key_grad,
        value_grad,
        mixing_grad,
        gains[1],
        gate_grad,
        up_grad,
        down_grad,
    )


def solution(mesh):
    in_specs = (
        P("dp", None),
        P(),
        P(),
        P(),
        P(None, "tensor"),
        P(None, "tensor"),
        P(None, "tensor"),
        P(None, "tensor"),
        P(),
        P(None, "tensor"),
        P(None, "tensor"),
        P(None, "tensor"),
        P("dp", None),
    )
    out_specs = (
        P(("dp", "tensor"), None),
        P(("dp", "tensor"), None),
        P(),
        P("dp", "tensor"),
        P("dp", "tensor"),
        P("dp", "tensor"),
        P("dp", "tensor"),
        P(),
        P("dp", "tensor"),
        P("dp", "tensor"),
        P("dp", "tensor"),
    )
    return jax.shard_map(
        on_device, mesh=mesh, in_specs=in_specs, out_specs=out_specs, check_vma=False
    )
```

profile of v0, /device:TPU:0, one launch (start us, length us, event | category | flops | bytes accessed | tf_op | source)
XLA Modules:
  0.0 243.4 jit_solution(18236980717414970859)
XLA Ops:
  0.6 1.3 reshape.30.refs_4_.refs_11_
  1.9 1.3 reshape.31.gain_ref.refs_12_
  3.2 26.4 %first.1 = (bf16[1024,1536]{1,0:T(8,128)(2,1)}, bf16[1024,1536]{1,0:T(8,128)(2,1)}, bf16[4,1024,96]{2,1,0:T(8,128)(2,1)}, bf16[4,1024,96]{2,1,0:T(8,128)(2,1)}, ...) custom-call(s32[12]{0:T(128)} %refs_0_.1, s32[12]{0:T(128)} %refs_1_.1, ...), custom_call_target="tpu_custom_call" | custom-call | tf_op jit(solution)/shard_map/first/pallas_call | solution.py:597
  29.7 57.1 %middle.1 = (f32[256,1536]{1,0:T(8,128)}, bf16[1024,1536]{1,0:T(8,128)(2,1)}, bf16[1024,1024]{1,0:T(8,128)(2,1)}, bf16[1024,1024]{1,0:T(8,128)(2,1)}, bf16[1024,...) custom-call(bf16[1024,384]{1,0:T(8,128)(2,1)} %get-tuple-element.44.o_ref.refs_17_, ...), custom_call_target="tpu_custom_call" | custom-call | tf_op jit(solution)/shard_map/middle/pallas_call | solution.py:393
  86.8 150.7 %back.1 = (bf16[256,1536]{1,0:T(8,128)(2,1)}, bf16[256,1536]{1,0:T(8,128)(2,1)}, f32[2,1536]{1,0:T(2,128)}, f32[192,1024]{1,0:T(8,128)}, f32[192,1024]{1,0:T(8,1...) custom-call(bf16[1024,1536]{1,0:T(8,128)(2,1)} %get-tuple-element.46.refs_0_, ...), custom_call_target="tpu_custom_call" | custom-call | tf_op jit(solution)/shard_map/back/pallas_call | solution.py:1359
  237.5 1.4 slice_reduce_fusion
  238.9 4.3 %last.1 = (bf16[256,1536]{1,0:T(8,128)(2,1)}, bf16[256,1536]{1,0:T(8,128)(2,1)}, f32[192,1024]{1,0:T(8,128)}, f32[192,1024]{1,0:T(8,128)}, f32[192,1024]{1,0:T(8...) custom-call(bf16[256,1536]{1,0:T(8,128)(2,1)} %get-tuple-element.59.refs_0_, ...), custom_call_target="tpu_custom_call" | custom-call | tf_op jit(solution)/shard_map/last/pallas_call | solution.py:700
where the time goes:
time: 244 us; the launch traced here: 243 us
  Pallas kernels  239 us (98%)
  local copies, waits for them, and re-layouts  4.01 us (2%)
    pallas_call x1, Pallas kernels, back_call(): pl.pallas_call(kernel, out_shape=(jax.ShapeDtypeStruct((rows, width), jnp...  151 us
    pallas_call x1, Pallas kernels, middle_call(): pl.pallas_call(middle_kernel, out_shape=(jax.ShapeDtypeStruct((rows, widt...  57.1 us
    pallas_call x1, Pallas kernels, first_call(): pl.pallas_call(kernel, grid=(blocks,), out_shape=(jax.ShapeDtypeStruct((s...  26.4 us

commit v1 on v0

--- a/solution.py
+++ b/solution.py
@@ -222,6 +222,7 @@
     load_sems,
     leave_sems,
     feed_buf,
+    grad_buf,
 ):
     index = lax.axis_index("tensor")
     rows = o_ref.shape[0] // 4
@@ -280,7 +281,7 @@
             cols = pl.ds(pl.multiple_of(i * columns, columns), columns)
             gate = nn(m_buf[there], gate_w[:, cols])
             upward = nn(m_buf[there], up_w[:, cols])
-            grad = nn(gm_buf[there], down_w[:, cols])
+            grad = grad_buf[there, cols]
             sigmoid = 1.0 / (1.0 + jnp.exp(-gate))
             activated = gate * sigmoid
             hid_buf[there, cols] = (activated * upward).astype(jnp.bfloat16)
@@ -325,13 +326,27 @@
     product(0)
     for c in range(SPLIT):
         reduce.arrive(0, 1, c)
-    loads[0].wait()
+    for i in (0, 3, 4):
+        loads[i].wait()
+    piece = grad_buf.shape[1] // SPLIT
+
+    def hidden_grad(c):
+        cols = pl.ds(c * piece, piece)
+
+        def some(i, carry):
+            there = span(i * 2 * rows, 2 * rows)
+            grad_buf[there, cols] = nn(gm_buf[there], down_w[:, cols])
+            return carry
+
+        lax.fori_loop(0, 2, some, 0)
+
     for c in range(SPLIT):
+        hidden_grad(c)
         reduce.arrive(1, 0, c, normed)
         gather.start(c)
     near = lax.div(index, 2)
     far = 1 - near
-    for load in loads[1:]:
+    for load in loads[1:3]:
         load.wait()
     for c in range(SPLIT):
         gather.near(c)
@@ -420,6 +435,7 @@
             pltpu.SemaphoreType.DMA((5,)),
             pltpu.SemaphoreType.DMA((12,)),
             low(slots, width),
+            pltpu.VMEM((slots, columns), jnp.float32),
         ],
         compiler_params=pltpu.CompilerParams(
             collective_id=0, has_side_effects=True, vmem_limit_bytes=67043328
@@ -428,7 +444,7 @@
     )(
         attended,
         mixing_weight,
-        second_gain.reshape(1, -1),
+        second_gain,
         tokens,
         outer_low,
         gate_weight,
@@ -439,6 +455,7 @@
 
 BLOCK = 256
 TILE = 384
+LOG2_E = float(np.log2(np.e))
 
 
 def head(index):
@@ -486,6 +503,7 @@
     x_ref,
     cot_ref,
     gain_ref,
+    next_gain_ref,
     wq_ref,
     wk_ref,
     wv_ref,
@@ -499,6 +517,8 @@
     lse_ref,
     begin_ref,
     used_ref,
+    gain_row,
+    next_row,
     kept,
     turned,
     o_heads,
@@ -514,6 +534,8 @@
         return total + length, begin
 
     used, begin = lax.fori_loop(0, lengths_ref.shape[0], sequence, (jnp.int32(0), slots))
+    gain_row[...] = gain_ref[...].reshape(1, -1)
+    next_row[...] = next_gain_ref[...].reshape(1, -1)
     begin_ref[...] = begin
     used_ref[0] = used
     size = 64
@@ -522,7 +544,7 @@
         rows = span(i * size, size)
         values = x_ref[rows].astype(jnp.float32)
         inverse = lax.rsqrt(jnp.mean(values * values, axis=-1, keepdims=True) + epsilon)
-        a_ref[rows] = (values * inverse * gain_ref[...]).astype(jnp.bfloat16)
+        a_ref[rows] = (values * inverse * gain_row[...]).astype(jnp.bfloat16)
         places = block * BLOCK + i * size + lax.broadcasted_iota(jnp.int32, (size, 1), 0)
         live = (places < used).astype(jnp.float32)
         gm_ref[rows] = (cot_ref[rows].astype(jnp.float32) * live).astype(jnp.bfloat16)
@@ -556,13 +578,14 @@
 
         def one_head(h, carry):
             group = lax.div(h, groups)
-            scores = nt(kept[group, pl.ds(0, stop)], q_ref[h]) * scaling
+            scores = nt(kept[group, pl.ds(0, stop)], q_ref[h])
             scores = jnp.where(allowed, scores, -jnp.inf)
             highest = jnp.max(scores, axis=0, keepdims=True)
-            exponent = jnp.exp(scores - highest)
+            exponent = jnp.exp2((scores - highest) * (scaling * LOG2_E))
             total = jnp.sum(exponent, axis=0, keepdims=True)
-            weights = (exponent * (1.0 / total)).astype(jnp.bfloat16)
-            mixed = nn(turned[group, :, pl.ds(0, stop)], weights)
+            weights = exponent.astype(jnp.bfloat16)
+            mixed = nn(turned[group, :, pl.ds(0, stop)], weights) * (1.0 / total)
+            highest = highest * scaling
             o_heads[h] = mixed.T.astype(jnp.bfloat16)
             lse_ref[pl.ds(h, 1)] = highest + jnp.log(total)
             return carry
@@ -576,7 +599,16 @@
 
 
 def first_call(
-    tokens, lengths, owners, first_gain, query_weight, key_weight, value_weight, cotangent, tables
+    tokens,
+    lengths,
+    owners,
+    first_gain,
+    second_gain,
+    query_weight,
+    key_weight,
+    value_weight,
+    cotangent,
+    tables,
 ):
     slots, width = tokens.shape
     blocks = slots // BLOCK
@@ -592,7 +624,8 @@
     def whole(array):
         return pl.BlockSpec(array.shape, lambda i: (0, 0), pipeline_mode=pl.Buffered(1))
 
-    gain = first_gain.reshape(1, -1)
+    whole_gain = pl.BlockSpec((width,), lambda i: (0,), pipeline_mode=pl.Buffered(1))
+    row = jax.ShapeDtypeStruct((1, width), jnp.float32)
     scalars = pl.BlockSpec(memory_space=pltpu.SMEM)
     return pl.pallas_call(
         kernel,
@@ -606,13 +639,16 @@
             jax.ShapeDtypeStruct((heads, slots), jnp.float32),
             jax.ShapeDtypeStruct((1, slots), jnp.int32),
             jax.ShapeDtypeStruct((1,), jnp.int32),
+            row,
+            row,
         ),
         in_specs=[
             scalars,
             scalars,
             rows_of(width),
             rows_of(width),
-            whole(gain),
+            whole_gain,
+            whole_gain,
             whole(query_weight),
             whole(key_weight),
             whole(value_weight),
@@ -628,6 +664,8 @@
             pl.BlockSpec((heads, BLOCK), lambda i: (0, i)),
             pl.BlockSpec((1, BLOCK), lambda i: (0, i)),
             scalars,
+            pl.BlockSpec((1, width), lambda i: (0, 0)),
+            pl.BlockSpec((1, width), lambda i: (0, 0)),
         ),
         scratch_shapes=[
             pltpu.VMEM((pairs // 2, slots, HD), jnp.bfloat16),
@@ -641,7 +679,8 @@
         owners,
         tokens,
         cotangent,
-        gain,
+        first_gain,
+        second_gain,
         query_weight,
         key_weight,
         value_weight,
@@ -650,8 +689,10 @@
 
 
 def last_kernel(group_columns, *refs):
-    sources, targets, buffers = refs[:8], refs[8:17], refs[17:28]
-    in_sems, out_sems = refs[28:]
+    sources, gains, targets, buffers = refs[:8], refs[8], refs[9:18], refs[20:31]
+    in_sems, out_sems = refs[31:]
+    for i, target in enumerate(refs[18:20]):
+        target[...] = gains[i]
     out, token, down, gate, up, mix, one, two = buffers[:8]
     turned = buffers[8:]
     coming = [
@@ -684,7 +725,7 @@
         copy.wait()
 
 
-def last_call(arrays, query_columns, key_columns):
+def last_call(arrays, gains, query_columns, key_columns):
     rows = arrays[6].shape[0]
     shapes = [jax.ShapeDtypeStruct(array.shape, array.dtype) for array in arrays[:6]]
     shapes += [
@@ -699,9 +740,9 @@
     buffers += [pltpu.VMEM(shape.shape, shape.dtype) for shape in shapes[6:]]
     return pl.pallas_call(
         kernel,
-        out_shape=tuple(shapes),
-        in_specs=[pl.BlockSpec(memory_space=pl.ANY)] * 8,
-        out_specs=tuple([pl.BlockSpec(memory_space=pl.ANY)] * 9),
+        out_shape=(*shapes, *([jax.ShapeDtypeStruct(gains.shape[1:], gains.dtype)] * 2)),
+        in_specs=[pl.BlockSpec(memory_space=pl.ANY)] * 8 + vmem_specs(1),
+        out_specs=(*([pl.BlockSpec(memory_space=pl.ANY)] * 9), *vmem_specs(2)),
         scratch_shapes=[
             *buffers,
             pltpu.SemaphoreType.DMA((8,)),
@@ -709,7 +750,7 @@
         ],
         compiler_params=pltpu.CompilerParams(vmem_limit_bytes=67043328),
         name="last",
-    )(*arrays)
+    )(*arrays, gains)
 
 
 def lanes(index):
@@ -1414,8 +1455,8 @@
         tokens,
         used,
         middle,
-        first_gain.reshape(1, -1),
-        second_gain.reshape(1, -1),
+        first_gain,
+        second_gain,
         mixing_weight,
         query_weight,
         key_weight,
@@ -1446,11 +1487,23 @@
 ):
     tables = rope_tables(tokens.shape[0])
     key_turned, value_turned = key_weight.T, value_weight.T
-    first_in, outer_low, queries, pairs, attended, log_totals, begin, used = first_call(
+    (
+        first_in,
+        outer_low,
+        queries,
+        pairs,
+        attended,
+        log_totals,
+        begin,
+        used,
+        first_row,
+        second_row,
+    ) = first_call(
         tokens,
         lengths,
         owners,
         first_gain,
+        second_gain,
         query_weight,
         key_turned,
         value_turned,
@@ -1460,7 +1513,7 @@
     middle, second_in, hidden, gate_low, upward_low, feed_part, second_part = middle_call(
         attended,
         mixing_weight,
-        second_gain,
+        second_row,
         tokens,
         outer_low,
         gate_weight,
@@ -1479,8 +1532,8 @@
         tokens,
         used,
         middle,
-        first_gain,
-        second_gain,
+        first_row,
+        second_row,
         mixing_weight,
         query_weight,
         key_turned,
@@ -1502,16 +1555,20 @@
         query_grad,
         key_grad,
         value_grad,
-    ) = last_call([layer_output, token_grad, *grads], query_weight.shape[1], key_weight.shape[1])
+        first_grad,
+        second_grad,
+    ) = last_call(
+        [layer_output, token_grad, *grads], gains, query_weight.shape[1], key_weight.shape[1]
+    )
     return (
         layer_output,
         token_grad,
-        gains[0],
+        first_grad,
         query_grad,
         key_grad,
         value_grad,
         mixing_grad,
-        gains[1],
+        second_grad,
         gate_grad,
         up_grad,
         down_grad,

time: 244 us -> 238 us (0.975)
  local copies, waits for them, and re-layouts: 4.01 us -> 0 us
    reshape x2 -> x0, local copies, waits for them, and re-layouts: 2.59 us -> none  [the longest x1 1.29 us: first_call(): gain = first_gain.reshape(1, -1)]
where the time goes in v1:
time: 238 us
  Pallas kernels  237 us (100%)
    pallas_call x1, Pallas kernels, back_call(): pl.pallas_call(kernel, out_shape=(jax.ShapeDtypeStruct((rows, width), jnp...  151 us
    pallas_call x1, Pallas kernels, middle_call(): pl.pallas_call(middle_kernel, out_shape=(jax.ShapeDtypeStruct((rows, widt...  56 us
    pallas_call x1, Pallas kernels, first_call(): pl.pallas_call(kernel, grid=(blocks,), out_shape=(jax.ShapeDtypeStruct((s...  24.8 us
    pallas_call x1, Pallas kernels, last_call(): pl.pallas_call(kernel, out_shape=(*shapes, *[jax.ShapeDtypeStruct(gains.s...  5.58 us

profile of v1, /device:TPU:0, one launch (start us, length us, event | category | flops | bytes accessed | tf_op | source)
XLA Modules:
  0.0 238.0 jit_solution(13958755609638576837)
XLA Ops:
  0.6 24.8 %first.1 = (bf16[1024,1536]{1,0:T(8,128)(2,1)}, bf16[1024,1536]{1,0:T(8,128)(2,1)}, bf16[4,1024,96]{2,1,0:T(8,128)(2,1)}, bf16[4,1024,96]{2,1,0:T(8,128)(2,1)}, ...) custom-call(s32[12]{0:T(128)} %refs_0_.1, ...), custom_call_target="tpu_custom_call" | custom-call | tf_op jit(solution)/shard_map/first/pallas_call | solution.py:630
  25.5 56.0 %middle.1 = (f32[256,1536]{1,0:T(8,128)}, bf16[1024,1536]{1,0:T(8,128)(2,1)}, bf16[1024,1024]{1,0:T(8,128)(2,1)}, bf16[1024,1024]{1,0:T(8,128)(2,1)}, bf16[1024,...) custom-call(bf16[1024,384]{1,0:T(8,128)(2,1)} %get-tuple-element.48.o_ref.refs_17_, ...), custom_call_target="tpu_custom_call" | custom-call | tf_op jit(solution)/shard_map/middle/pallas_call | solution.py:408
  81.5 150.7 %back.1 = (bf16[256,1536]{1,0:T(8,128)(2,1)}, bf16[256,1536]{1,0:T(8,128)(2,1)}, f32[2,1536]{1,0:T(2,128)}, f32[192,1024]{1,0:T(8,128)}, f32[192,1024]{1,0:T(8,1...) custom-call(bf16[1024,1536]{1,0:T(8,128)(2,1)} %get-tuple-element.51.refs_0_, ...), custom_call_target="tpu_custom_call" | custom-call | tf_op jit(solution)/shard_map/back/pallas_call | solution.py:1400
  232.2 5.6 %last.1 = (bf16[256,1536]{1,0:T(8,128)(2,1)}, bf16[256,1536]{1,0:T(8,128)(2,1)}, f32[192,1024]{1,0:T(8,128)}, f32[192,1024]{1,0:T(8,128)}, f32[192,1024]{1,0:T(8...) custom-call(bf16[256,1536]{1,0:T(8,128)(2,1)} %get-tuple-element.65., ...), custom_call_target="tpu_custom_call" | custom-call | tf_op jit(solution)/shard_map/last/pallas_call | solution.py:741

commit v2 on v1

--- a/solution.py
+++ b/solution.py
@@ -810,87 +810,87 @@
     (P_TILE, P_GATE, 3),
     (P_TILE, P_DOWN, 3),
     (P_START, P_DM),
+    (P_ARRIVE, P_DM, 0, 0, 1),
     (P_TILE, P_GATE, 1),
-    (P_ARRIVE, P_DM, 0, 0, 2),
-    (P_ARRIVE, P_DM, 0, 1, 1),
-    (P_ARRIVE, P_DM, 0, 1, 0),
-    (P_ARRIVE, P_DM, 0, 0, 0),
     (P_TILE, P_DOWN, 1),
     (P_TILE, P_GATE, 2),
-    (P_ARRIVE, P_DM, 0, 0, 1),
+    (P_ARRIVE, P_DM, 0, 0, 2),
+    (P_ARRIVE, P_GATE, 0, 0, 0),
+    (P_ARRIVE, P_DM, 0, 0, 0),
+    (P_ARRIVE, P_DM, 0, 1, 1),
+    (P_ARRIVE, P_DM, 0, 1, 3),
+    (P_ARRIVE, P_DM, 0, 0, 3),
+    (P_ARRIVE, P_GATE, 0, 1, 0),
     (P_TILE, P_DOWN, 2),
-    (P_ARRIVE, P_DM, 0, 1, 3),
+    (P_ARRIVE, P_DOWN, 0, 0, 0),
+    (P_ARRIVE, P_DM, 0, 1, 0),
+    (P_TILE, P_GATE, 0),
+    (P_ARRIVE, P_DM, 0, 1, 2),
+    (P_TILE, P_DOWN, 0),
+    (P_TILE, P_UP, 3),
     (P_ARRIVE, P_DM, 1, 0, 1),
-    (P_ARRIVE, P_DM, 0, 1, 2),
-    (P_ARRIVE, P_DM, 0, 0, 3),
-    (P_ARRIVE, P_GATE, 0, 0, 0),
-    (P_TILE, P_GATE, 0),
-    (P_ARRIVE, P_GATE, 0, 1, 0),
+    (P_ARRIVE, P_DM, 1, 0, 0),
+    (P_ARRIVE, P_GATE, 0, 2, 0),
     (P_FORWARD, 1),
-    (P_TILE, P_DOWN, 0),
+    (P_ARRIVE, P_DM, 1, 0, 2),
+    (P_FINISH, 1),
     (P_ARRIVE, P_DOWN, 0, 2, 0),
-    (P_ARRIVE, P_GATE, 0, 2, 0),
-    (P_ARRIVE, P_DOWN, 0, 0, 0),
-    (P_ARRIVE, P_DM, 1, 0, 2),
-    (P_TILE, P_UP, 3),
-    (P_ARRIVE, P_DM, 1, 0, 0),
+    (P_FORWARD, 0),
+    (P_ARRIVE, P_DM, 1, 0, 3),
     (P_TILE, P_UP, 1),
-    (P_FINISH, 1),
     (P_TILE, P_UP, 2),
-    (P_ARRIVE, P_DM, 1, 0, 3),
-    (P_FORWARD, 0),
     (P_TILE, P_UP, 0),
-    (P_ARRIVE, P_DOWN, 0, 1, 0),
-    (P_FORWARD, 2),
     (P_ARRIVE, P_GATE, 0, 3, 0),
     (P_FINISH, 0),
+    (P_ARRIVE, P_DOWN, 1, 0, 0),
+    (P_FORWARD, 2),
+    (P_FINISH, 2),
     (P_FORWARD, 3),
     (P_FINISH, 3),
-    (P_ARRIVE, P_DOWN, 1, 0, 0),
-    (P_FINISH, 2),
     (P_START, P_FEED),
+    (P_TILE, P_MIX, 3),
     (P_ARRIVE, P_FEED, 0, 0, 0),
-    (P_TILE, P_MIX, 3),
-    (P_ARRIVE, P_FEED, 0, 0, 1),
-    (P_ARRIVE, P_FEED, 0, 0, 2),
     (P_TILE, P_MIX, 1),
     (P_TILE, P_MIX, 2),
     (P_TILE, P_MIX, 0),
+    (P_BACK,),
+    (P_ARRIVE, P_FEED, 0, 0, 1),
+    (P_ATTENTION, 0, 3),
+    (P_ARRIVE, P_FEED, 0, 1, 2),
+    (P_ARRIVE, P_UP, 0, 0, 0),
     (P_ARRIVE, P_FEED, 0, 1, 1),
     (P_ARRIVE, P_FEED, 0, 0, 3),
-    (P_ARRIVE, P_UP, 0, 0, 0),
+    (P_ARRIVE, P_GATE, 1, 1, 0),
     (P_ARRIVE, P_GATE, 1, 0, 0),
-    (P_BACK,),
-    (P_ARRIVE, P_FEED, 1, 0, 1),
-    (P_ATTENTION, 0, 3),
     (P_ARRIVE, P_UP, 0, 1, 0),
     (P_ARRIVE, P_FEED, 0, 1, 0),
-    (P_ARRIVE, P_DOWN, 0, 3, 0),
+    (P_ARRIVE, P_FEED, 0, 1, 3),
     (P_ATTENTION, 0, 2),
     (P_ATTENTION, 0, 1),
+    (P_ARRIVE, P_FEED, 1, 0, 1),
     (P_ATTENTION, 0, 0),
+    (P_ARRIVE, P_FEED, 0, 0, 2),
+    (P_ARRIVE, P_DOWN, 0, 1, 0),
+    (P_ARRIVE, P_DOWN, 0, 3, 0),
+    (P_ARRIVE, P_UP, 0, 2, 0),
+    (P_ARRIVE, P_FEED, 1, 0, 0),
     (P_KEYS, 0),
-    (P_ARRIVE, P_FEED, 1, 0, 0),
     (P_TILE, P_ONE, 3),
     (P_TILE, P_ONE, 1),
-    (P_ARRIVE, P_GATE, 1, 1, 0),
     (P_TILE, P_ONE, 2),
     (P_TILE, P_ONE, 0),
-    (P_ARRIVE, P_FEED, 0, 1, 2),
-    (P_ARRIVE, P_FEED, 1, 0, 2),
     (P_ATTENTION, 1, 3),
     (P_ATTENTION, 1, 2),
-    (P_ARRIVE, P_FEED, 0, 1, 3),
-    (P_ARRIVE, P_UP, 0, 2, 0),
-    (P_ARRIVE, P_FEED, 1, 0, 3),
+    (P_ARRIVE, P_MIX, 0, 0, 0),
     (P_ATTENTION, 1, 1),
     (P_ATTENTION, 1, 0),
-    (P_ARRIVE, P_MIX, 0, 0, 0),
     (P_ARRIVE, P_UP, 1, 0, 0),
+    (P_ARRIVE, P_FEED, 1, 0, 2),
     (P_ARRIVE, P_GATE, 2, 0, 0),
+    (P_ARRIVE, P_MIX, 0, 2, 0),
+    (P_ARRIVE, P_UP, 0, 3, 0),
+    (P_ARRIVE, P_FEED, 1, 0, 3),
     (P_KEYS, 1),
-    (P_ARRIVE, P_DOWN, 1, 1, 0),
-    (P_ARRIVE, P_DOWN, 2, 0, 0),
     (P_TILE, P_TWO, 3),
     (P_TILE, P_TWO, 1),
     (P_TILE, P_TWO, 2),
@@ -899,48 +899,48 @@
     (P_PRODUCT, 1),
     (P_PRODUCT, 2),
     (P_ARRIVE, P_DA, 0, 0, 1),
+    (P_ARRIVE, P_DA, 0, 0, 2),
+    (P_ARRIVE, P_MIX, 0, 1, 0),
     (P_PRODUCT, 0),
-    (P_ARRIVE, P_DA, 0, 1, 1),
+    (P_ARRIVE, P_DOWN, 1, 1, 0),
+    (P_ARRIVE, P_DA, 0, 0, 3),
+    (P_ARRIVE, P_ONE, 0, 0, 0),
     (P_ARRIVE, P_DA, 0, 0, 0),
-    (P_ARRIVE, P_MIX, 0, 1, 0),
-    (P_ARRIVE, P_DA, 0, 0, 3),
-    (P_ARRIVE, P_UP, 0, 3, 0),
+    (P_ARRIVE, P_ONE, 0, 1, 0),
+    (P_ARRIVE, P_UP, 1, 1, 0),
     (P_ARRIVE, P_DA, 0, 1, 0),
-    (P_ARRIVE, P_ONE, 0, 0, 0),
+    (P_ARRIVE, P_MIX, 1, 0, 0),
+    (P_ARRIVE, P_ONE, 0, 3, 0),
     (P_ARRIVE, P_DA, 0, 1, 2),
-    (P_ARRIVE, P_MIX, 0, 2, 0),
-    (P_ARRIVE, P_DA, 1, 0, 0),
-    (P_ARRIVE, P_MIX, 0, 3, 0),
-    (P_ARRIVE, P_MIX, 1, 0, 0),
-    (P_ARRIVE, P_DA, 0, 0, 2),
-    (P_ARRIVE, P_DA, 1, 0, 1),
-    (P_ARRIVE, P_ONE, 0, 1, 0),
+    (P_ARRIVE, P_TWO, 0, 0, 0),
     (P_ARRIVE, P_ONE, 0, 2, 0),
-    (P_ARRIVE, P_TWO, 0, 0, 0),
-    (P_ARRIVE, P_MIX, 1, 1, 0),
-    (P_ARRIVE, P_TWO, 0, 1, 0),
-    (P_ARRIVE, P_DA, 1, 0, 2),
-    (P_ARRIVE, P_UP, 1, 1, 0),
     (P_ARRIVE, P_DA, 0, 1, 3),
     (P_ARRIVE, P_DA, 1, 0, 3),
+    (P_ARRIVE, P_DA, 0, 1, 1),
+    (P_ARRIVE, P_DA, 1, 0, 1),
+    (P_ARRIVE, P_TWO, 0, 1, 0),
+    (P_ARRIVE, P_MIX, 0, 3, 0),
+    (P_ARRIVE, P_DA, 1, 0, 0),
+    (P_ARRIVE, P_DA, 1, 0, 2),
     (P_SEND, 0),
-    (P_ARRIVE, P_TWO, 0, 2, 0),
     (P_ADD, 0),
     (P_ARRIVE, P_ONE, 1, 0, 0),
-    (P_ARRIVE, P_UP, 2, 0, 0),
+    (P_ARRIVE, P_DOWN, 2, 0, 0),
+    (P_ARRIVE, P_TWO, 0, 2, 0),
     (P_SEND, 1),
     (P_ADD, 1),
     (P_SEND, 2),
     (P_ADD, 2),
     (P_SEND, 3),
     (P_ARRIVE, P_TWO, 1, 0, 0),
+    (P_ARRIVE, P_MIX, 1, 1, 0),
     (P_ADD, 3),
-    (P_ARRIVE, P_ONE, 0, 3, 0),
+    (P_ARRIVE, P_UP, 2, 0, 0),
+    (P_ARRIVE, P_ONE, 1, 1, 0),
+    (P_ARRIVE, P_ONE, 2, 0, 0),
     (P_ARRIVE, P_MIX, 2, 0, 0),
     (P_ARRIVE, P_TWO, 0, 3, 0),
     (P_ARRIVE, P_TWO, 1, 1, 0),
-    (P_ARRIVE, P_ONE, 1, 1, 0),
-    (P_ARRIVE, P_ONE, 2, 0, 0),
     (P_SEND, 4),
     (P_ARRIVE, P_TWO, 2, 0, 0),
     (P_ADD, 4),
@@ -1184,6 +1184,7 @@
     }
     peers = TENSOR_PEERS + tuple(("dp", bit) for bit in dp_order)
     gains = []
+    ended = []
     turned = {}
 
     def turned_back(values, block):
@@ -1227,7 +1228,8 @@
             reduce.arrive(step, j, c, {"dm": finish_dm, "feed": finish_out, "da": finish_da}[name])
             if name == "dm":
                 gather.start(c)
-            if name == "feed" and c == SPLIT - 1:
+            ended.append(name)
+            if name == "feed" and ended.count(name) == SPLIT:
                 for mask in (1, 2):
                     pl.semaphore_signal(
                         credit,
@@ -1237,7 +1239,7 @@
                     )
                 feed.close()
                 out_copy.start()
-            if name == "da" and c == SPLIT - 1:
+            if name == "da" and ended.count(name) == SPLIT:
                 token_copy.start()
 
     def do_back():

time: 238 us -> 237 us (level)
  no operation moved by 1% of the time
where the time goes in v2:
time: 237 us
  Pallas kernels  236 us (100%)
    pallas_call x1, Pallas kernels, back_call(): pl.pallas_call(kernel, out_shape=(jax.ShapeDtypeStruct((rows, width), jnp...  150 us
    pallas_call x1, Pallas kernels, middle_call(): pl.pallas_call(middle_kernel, out_shape=(jax.ShapeDtypeStruct((rows, widt...  56 us
    pallas_call x1, Pallas kernels, first_call(): pl.pallas_call(kernel, grid=(blocks,), out_shape=(jax.ShapeDtypeStruct((s...  24.8 us
    pallas_call x1, Pallas kernels, last_call(): pl.pallas_call(kernel, out_shape=(*shapes, *[jax.ShapeDtypeStruct(gains.s...  5.58 us

profile of v2, /device:TPU:0, one launch (start us, length us, event | category | flops | bytes accessed | tf_op | source)
XLA Modules:
  0.0 236.9 jit_solution(4763478455711482099)
XLA Ops:
  0.6 24.8 %first.1 = (bf16[1024,1536]{1,0:T(8,128)(2,1)}, bf16[1024,1536]{1,0:T(8,128)(2,1)}, bf16[4,1024,96]{2,1,0:T(8,128)(2,1)}, bf16[4,1024,96]{2,1,0:T(8,128)(2,1)}, ...) custom-call(s32[12]{0:T(128)} %refs_0_.1, ...), custom_call_target="tpu_custom_call" | custom-call | tf_op jit(solution)/shard_map/first/pallas_call | solution.py:630
  25.5 56.0 %middle.1 = (f32[256,1536]{1,0:T(8,128)}, bf16[1024,1536]{1,0:T(8,128)(2,1)}, bf16[1024,1024]{1,0:T(8,128)(2,1)}, bf16[1024,1024]{1,0:T(8,128)(2,1)}, bf16[1024,...) custom-call(bf16[1024,384]{1,0:T(8,128)(2,1)} %get-tuple-element.48.o_ref.refs_17_, ...), custom_call_target="tpu_custom_call" | custom-call | tf_op jit(solution)/shard_map/middle/pallas_call | solution.py:408
  81.5 149.6 %back.1 = (bf16[256,1536]{1,0:T(8,128)(2,1)}, bf16[256,1536]{1,0:T(8,128)(2,1)}, f32[2,1536]{1,0:T(2,128)}, f32[192,1024]{1,0:T(8,128)}, f32[192,1024]{1,0:T(8,1...) custom-call(bf16[1024,1536]{1,0:T(8,128)(2,1)} %get-tuple-element.51.refs_0_, ...), custom_call_target="tpu_custom_call" | custom-call | tf_op jit(solution)/shard_map/back/pallas_call | solution.py:1402
  231.2 5.6 %last.1 = (bf16[256,1536]{1,0:T(8,128)(2,1)}, bf16[256,1536]{1,0:T(8,128)(2,1)}, f32[192,1024]{1,0:T(8,128)}, f32[192,1024]{1,0:T(8,128)}, f32[192,1024]{1,0:T(8...) custom-call(bf16[256,1536]{1,0:T(8,128)(2,1)} %get-tuple-element.65., ...), custom_call_target="tpu_custom_call" | custom-call | tf_op jit(solution)/shard_map/last/pallas_call | solution.py:741
